TPU v7x, 256 devices: a whole 4x4x8 slice. The times are simulated.
256 devices in a mesh: grp: 4 (over y), dev: 64 (over z, x, core).
Axes of the slice: x: 4, y: 4, z: 8, core: 2. Of those that a mesh axis runs over, the one named last changes fastest.
Arguments:
- nz_user: int32 [32768, 128], P(('grp', 'dev')), may hold values from 0 to 65535
- nz_sub: int32 [32768, 128], P(('grp', 'dev')), may hold values from 0 to 16383
- nz_value: float32 [32768, 128], P(('grp', 'dev')), may hold values from -1 to 1
- tile_word: int32 [32768], P(('grp', 'dev')), may hold values from 0 to 16383, as said below
- word_owner: int32 [16384], replicated, may hold values from 0 to 16383, as said below
- user_factor: bfloat16 [64, 65536], P(None, 'dev'), may hold values from -6 to 6
- sub_factor: bfloat16 [64, 16384], P(None, 'dev'), may hold values from -6 to 6
Outputs:
- word_rows: float32 [64, 16384], P(None, ('grp', 'dev'))
Inputs may be any that keep to these rules, and one draw needn't show every extreme that they name: A permutation of the word indices: word w is summed into column word_owner[w] of word_rows. `tile_word`: tile i lies on device i // 128 (grp+dev order). On every device at most 2 tiles belong to words whose output column lies on any one other device, and on every device that bound is reached for some other device.
All inputs are finite; a program needn't handle non-finite values.
Results may differ from a plain program's by a relative error of at most 0.0003.
Values may be sent and summed in bfloat16 or wider, within the bound.
No kernel may reach another device: no remote copies, remote signals or barrier semaphores. Data moves between devices by JAX's collectives and lax.ppermute only.
A program may use at most 64 MiB of HBM per device.

v0:
```python
import jax
import jax.numpy as jnp
from jax import lax
from jax.sharding import PartitionSpec as P

CAP = 2


def cut_along(value, dim, peers):
    shape = value.shape
    pieces = value.reshape(*shape[:dim], peers, shape[dim] // peers, *shape[dim + 1 :])
    return jnp.moveaxis(pieces, dim, 0)


def joined_along(pieces, dim):
    pieces = jnp.moveaxis(pieces, 0, dim)
    shape = pieces.shape
    return pieces.reshape(*shape[:dim], shape[dim] * shape[dim + 1], *shape[dim + 2 :])


def exchange_both(value, axis, axes, splits, concats):
    sizes = [lax.axis_size(a) for a in axes]
    pieces = cut_along(value, splits[0], sizes[0])
    pieces = jnp.moveaxis(cut_along(pieces, splits[1] + 1, sizes[1]), 0, 1)
    inside = pieces.shape[2:]
    pieces = pieces.reshape(-1, *inside)
    pieces = lax.all_to_all(pieces, axis, split_axis=0, concat_axis=0, tiled=True)
    pieces = joined_along(pieces.reshape(*sizes, *inside), concats[0] + 1)
    return joined_along(pieces, concats[1])


def tile_sums(user_table, sub_table, nz_user, nz_sub, nz_value):
    tile_count, tile_width = nz_user.shape
    block_tiles = min(tile_count, 128)
    block_count = tile_count // block_tiles

    def one_block(block_args):
        users_block, subs_block, vals_block = block_args
        user_rows = jnp.take(user_table, users_block, axis=0).astype(jnp.float32)
        sub_rows = jnp.take(sub_table, subs_block, axis=0).astype(jnp.float32)
        return jnp.sum(user_rows * sub_rows * vals_block[:, :, None], axis=1)

    block_sums = lax.map(
        one_block,
        (
            nz_user.reshape(block_count, block_tiles, tile_width),
            nz_sub.reshape(block_count, block_tiles, tile_width),
            nz_value.reshape(block_count, block_tiles, tile_width),
        ),
    )
    return block_sums.reshape(tile_count, block_sums.shape[2])


def shards(nz_user, nz_sub, nz_value, tile_word, word_owner, user_factor, sub_factor):
    users_all, subs_all = (
        lax.all_gather(user_factor, "dev", axis=1, tiled=True),
        lax.all_gather(sub_factor, "dev", axis=1, tiled=True),
    )
    user_table = jnp.transpose(users_all)
    sub_table = jnp.transpose(subs_all)
    tile_rows = tile_sums(user_table, sub_table, nz_user, nz_sub, nz_value)
    tile_count, rank_width = tile_rows.shape
    grp_size = lax.axis_size("grp")
    dev_size = lax.axis_size("dev")
    devices_all = grp_size * dev_size
    words_total = word_owner.shape[0]
    words_local = words_total // devices_all
    out_rows = jnp.take(word_owner, tile_word)
    self_index = lax.axis_index("grp") * dev_size + lax.axis_index("dev")
    owner_dev = out_rows // words_local
    local_row = out_rows - owner_dev * words_local
    owned = owner_dev == self_index
    columns = jnp.arange(words_local, dtype=jnp.int32)
    own_table = (owned[:, None] & (local_row[:, None] == columns[None, :])).astype(jnp.float32)
    own_part = jnp.einsum("tr,tk->rk", tile_rows, own_table, precision=lax.Precision.HIGHEST)
    peer_ids = jnp.arange(devices_all, dtype=jnp.int32)
    outgoing = (jnp.logical_not(owned)[:, None] & (owner_dev[:, None] == peer_ids[None, :])).astype(
        jnp.float32
    )
    tile_ids = jnp.arange(tile_count, dtype=jnp.int32)
    earlier_table = (tile_ids[:, None] > tile_ids[None, :]).astype(jnp.float32)
    earlier = jnp.dot(
        earlier_table, outgoing, precision=lax.Precision.HIGHEST, preferred_element_type=jnp.float32
    )
    position = jnp.sum(earlier * outgoing, axis=1).astype(jnp.int32)
    send_slot = jnp.where(owned, devices_all * CAP, owner_dev * CAP + position)
    slot_ids = jnp.arange(devices_all * CAP, dtype=jnp.int32)
    slot_table = (send_slot[:, None] == slot_ids[None, :]).astype(jnp.float32)
    send_rows = jnp.einsum("ts,tr->sr", slot_table, tile_rows, precision=lax.Precision.HIGHEST)
    filled = jnp.sum(slot_table, axis=0)
    send_ids = (
        jnp.dot(
            local_row.astype(jnp.float32),
            slot_table,
            precision=lax.Precision.HIGHEST,
            preferred_element_type=jnp.float32,
        )
        + filled
        - 1.0
    )
    send_rows = send_rows.reshape(grp_size, dev_size, CAP * rank_width)
    send_ids = send_ids.reshape(grp_size, dev_size, CAP)
    got_rows, got_ids = (
        exchange_both(send_rows, ("dev", "grp"), ("dev", "grp"), (1, 0), (1, 0)),
        exchange_both(send_ids, ("dev", "grp"), ("dev", "grp"), (1, 0), (1, 0)),
    )
    got_rows = got_rows.reshape(devices_all * CAP, rank_width)
    got_ids = got_ids.reshape(devices_all * CAP).astype(jnp.int32)
    got_table = (got_ids[:, None] == columns[None, :]).astype(jnp.float32)
    far_part = jnp.einsum("sr,sk->rk", got_rows, got_table, precision=lax.Precision.HIGHEST)
    return own_part + far_part


def solution(mesh):
    return jax.shard_map(
        shards,
        mesh=mesh,
        in_specs=(
            P(("grp", "dev"), None),
            P(("grp", "dev"), None),
            P(("grp", "dev"), None),
            P(("grp", "dev")),
            P(),
            P(None, "dev"),
            P(None, "dev"),
        ),
        out_specs=P(None, ("grp", "dev")),
        check_vma=False,
    )
```

profile of v0, /device:TPU:1, one launch (start us, length us, event | category | flops | bytes accessed | tf_op | source)
XLA Modules:
  0.0 297.3 jit_solution(12197286190946821888)
XLA Ops:
  6.5 1.5 copy.45
  8.1 1.8 copy.44
  9.9 0.7 compare_select_fusion.2
  10.6 1.1 gather_fusion.2
  11.8 0.7 fusion.17
  12.4 0.3 fusion
  12.8 0.7 add_select_fusion
  14.0 0.7 copy.55
  14.7 15.6 %all-to-all-start.1 = ((f32[256,1,1,2]{3,2,1,0:T(1,128)}), f32[256,1,1,2]{3,2,1,0:T(1,128)S(1)}, u32[]{:S(2)}, u32[]{:S(2)}) async-start(f32[256,1,1,2]{3,2,1,0:T(1,128)} %bitcast.14), calls=%async_computation.1 | async-start | bytes 262144 | tf_op jit(solution)/shard_map/all_to_all | solution.py:27
  30.4 0.9 compare_and_fusion
  31.3 0.9 bitcast_clamp_fusion.1
  32.1 0.9 bitcast_clamp_fusion
  33.0 60.6 %all-gather.5.cloned.1.call-done = bf16[64,16384]{0,1:T(8,128)(2,1)} async-done(((bf16[64,256]{0,1:T(8,128)(2,1)}), bf16[64,16384]{0,1:T(8,128)(2,1)}) %all-gather.5.cloned.1.call-update) | async-done | bytes 2097168 | tf_op jit(solution)/shard_map/all_gather | solution.py:57
  93.6 58.1 %gather_fusion.1 = bf16[16384,64]{1,0:T(8,128)(2,1)} fusion(bf16[16384,64]{1,0:T(8,128)(2,1)} %bitcast.38, s32[16384]{0:T(1024)S(1)} %bitcast_clamp_fusion), kind=kCustom, calls=%fused_computation.1 | custom fusion | bytes 4259840 | tf_op jit(solution)/shard_map/while/body/eval_jaxpr/jit(_take)/gather | solution.py:40
  151.8 41.1 %all-gather.3.cloned.1.call-done = bf16[64,65536]{0,1:T(8,128)(2,1)} async-done(((bf16[64,1024]{0,1:T(8,128)(2,1)}), bf16[64,65536]{0,1:T(8,128)(2,1)}) %all-gather.3.cloned.1.call-update) | async-done | bytes 8388624 | tf_op jit(solution)/shard_map/all_gather | solution.py:56
  192.8 63.3 %gather_fusion = bf16[16384,64]{1,0:T(8,128)(2,1)} fusion(bf16[65536,64]{1,0:T(8,128)(2,1)} %bitcast.39, s32[16384]{0:T(1024)S(1)} %bitcast_clamp_fusion.1), kind=kCustom, calls=%fused_computation | custom fusion | bytes 4259840 | tf_op jit(solution)/shard_map/while/body/eval_jaxpr/jit(_take)/gather | solution.py:39
  256.2 10.6 %multiply_reduce_fusion = f32[128,64]{1,0:T(8,128)S(1)} fusion(f32[128,128]{1,0:T(8,128)S(1)} %copy-done.1, pred[128,128]{1,0:T(8,128)(4,1)S(1)} %get-tuple-element.30, pred[128,128]{1,0:T(8,128)(4,1)S(1)} %get-tuple-element.32, bf16[16384,64]{1,0:T(8,128)(2,1)} %gather_fusion.1, bf16[16384,64]{1,0:T(8,128)(2,1)} %gather_fusion), kind=kLoop, calls=%fused_computation.3 | loop fusion | flops 7331840 | bytes 4325376 | tf_op jit(solution)/shard_map/while/body/eval_jaxpr/reduce_sum | solution.py:41
  266.8 0.5 fusion.2
  267.3 0.7 copy.47
  268.1 8.5 %all-to-all-start = ((f32[256,1,1,128]{3,2,1,0:T(1,128)}), f32[256,1,1,128]{3,2,1,0:T(1,128)S(1)}, u32[]{:S(2)}, u32[]{:S(2)}) async-start(f32[256,1,1,128]{3,2,1,0:T(1,128)} %bitcast.8), calls=%async_computation | async-start | bytes 262144 | tf_op jit(solution)/shard_map/all_to_all | solution.py:27
  276.8 0.6 copy.53
  277.5 0.3 fusion.11
  277.8 11.5 %all-to-all-done = f32[256,1,1,128]{3,2,1,0:T(1,128)S(1)} async-done(((f32[256,1,1,128]{3,2,1,0:T(1,128)}), f32[256,1,1,128]{3,2,1,0:T(1,128)S(1)}, u32[]{:S(2)}, u32[]{:S(2)}) %all-to-all-start) | async-done | bytes 131104 | tf_op jit(solution)/shard_map/all_to_all | solution.py:27
  289.4 1.1 convolution_add_fusion
  (21 shorter events, 1.2 us)
Async XLA Ops:
  6.5 4.1 %copy-start = (s32[16384]{0:T(1024)S(1)}, s32[16384]{0:T(1024)}, u32[]{:S(2)}) copy-start(s32[16384]{0:T(1024)} %param.11) | copy-start | bytes 196612
  6.5 87.1 %all-gather.5.cloned.1.call-start = ((), (), s32[]{:S(2)}) async-start(), calls=%async_computation.3 | async-start | bytes 4259840 | tf_op jit(solution)/shard_map/all_gather | solution.py:57
  8.1 184.8 %all-gather.3.cloned.1.call-start = ((), (), s32[]{:S(2)}) async-start(), calls=%async_computation.2 | async-start | bytes 17039360 | tf_op jit(solution)/shard_map/all_gather | solution.py:56
  14.7 253.4 %all-to-all-start.1 = ((f32[256,1,1,2]{3,2,1,0:T(1,128)}), f32[256,1,1,2]{3,2,1,0:T(1,128)S(1)}, u32[]{:S(2)}, u32[]{:S(2)}) async-start(f32[256,1,1,2]{3,2,1,0:T(1,128)} %bitcast.14), calls=%async_computation.1 | async-start | bytes 262144 | tf_op jit(solution)/shard_map/all_to_all | solution.py:27
  192.8 63.3 %copy-start.1 = (f32[128,128]{1,0:T(8,128)S(1)}, f32[128,128]{1,0:T(8,128)}, u32[]{:S(2)}) copy-start(f32[128,128]{1,0:T(8,128)} %param.9) | copy-start | bytes 196612
  268.1 21.2 %all-to-all-start = ((f32[256,1,1,128]{3,2,1,0:T(1,128)}), f32[256,1,1,128]{3,2,1,0:T(1,128)S(1)}, u32[]{:S(2)}, u32[]{:S(2)}) async-start(f32[256,1,1,128]{3,2,1,0:T(1,128)} %bitcast.8), calls=%async_computation | async-start | bytes 262144 | tf_op jit(solution)/shard_map/all_to_all | solution.py:27
Sparse Core Ops, SparseCore 0:
  10.1 83.5 all-gather.4
  96.4 96.3 all-gather.2
where the time goes:
time: 298 us; the launch traced here: 297 us
  local copies, waits for them, and re-layouts  129 us (43%)
  waiting for transfers between devices  113 us (38%)
  starting transfers between devices  24.2 us (8%)
  other arithmetic  15.4 us (5%)
  between operations  13.5 us (5%)
    gather x1, local copies, waits for them, and re-layouts, one_block(): user_rows = jnp.take(user_table, users_block, axis=0).astype(jnp.float32)  63.3 us
    all_gather x1, waiting for transfers between devices, shards(): lax.all_gather(sub_factor, 'dev', axis=1, tiled=True)  60.6 us
    gather x1, local copies, waits for them, and re-layouts, one_block(): sub_rows = jnp.take(sub_table, subs_block, axis=0).astype(jnp.float32)  58.1 us
    all_gather x1, waiting for transfers between devices, shards(): lax.all_gather(user_factor, 'dev', axis=1, tiled=True)  41.1 us
    all_to_all x2, starting transfers between devices, exchange_both(): lax.all_to_all(pieces, axis, split_axis=0, concat_axis=0, tiled=True)  24.1 us
    all_to_all x2, waiting for transfers between devices, exchange_both(): lax.all_to_all(pieces, axis, split_axis=0, concat_axis=0, tiled=True)  11.5 us
    reduce_sum x1, other arithmetic, one_block(): return jnp.sum(user_rows * sub_rows * vals_block[:, :, None], axis=1)  10.6 us
  transfers between devices with their start and end apart: 4, of which 3 were waited for; matrix products, arithmetic and copies ran while one was open for 48% of the time, Pallas kernels for 0%

commit v1 on v0

--- a/solution.py
+++ b/solution.py
@@ -2,8 +2,12 @@
 import jax.numpy as jnp
 from jax import lax
 from jax.sharding import PartitionSpec as P
+from jax.lax import all_to_all, axis_size
 
 CAP = 2
+open_run = lambda where_dim, piece_in: jnp.concatenate(
+    all_to_all(jnp.stack([piece_in] * axis_size("dev"), axis=0), "dev", 0, 0), where_dim
+)
 
 
 def cut_along(value, dim, peers):
@@ -53,7 +57,7 @@
 
 def shards(nz_user, nz_sub, nz_value, tile_word, word_owner, user_factor, sub_factor):
     users_all, subs_all = (
-        lax.all_gather(user_factor, "dev", axis=1, tiled=True),
+        open_run(1, user_factor),
         lax.all_gather(sub_factor, "dev", axis=1, tiled=True),
     )
     user_table = jnp.transpose(users_all)

time: 298 us -> 358 us (1.20)
  waiting for transfers between devices: 113 us -> 145 us
  local copies, waits for them, and re-layouts: 129 us -> 146 us
  starting transfers between devices: 24.2 us -> 39.6 us
  other arithmetic: 15.4 us -> 10.8 us
    all_gather x1, waiting for transfers between devices: 60.6 us -> 112 us  [shards(): lax.all_gather(sub_factor, 'dev', axis=1, tiled=True)]
    all_gather x1 -> x0, waiting for transfers between devices: 41.1 us -> none  [shards(): lax.all_gather(user_factor, 'dev', axis=1, tiled=True)]
    all_to_all x0 -> x1, waiting for transfers between devices: none -> 21.1 us  [all_to_all(jnp.stack([piece_in] * axis_size('dev'), axis=0), 'dev', 0, 0)]
    reshape x0 -> x1, local copies, waits for them, and re-layouts: none -> 15.5 us  [jnp.concatenate(all_to_all(jnp.stack([piece_in] * axis_size('dev'), axis=...]
    all_to_all x0 -> x1, starting transfers between devices: none -> 13.3 us  [all_to_all(jnp.stack([piece_in] * axis_size('dev'), axis=0), 'dev', 0, 0)]
    another operation x0 -> x1, local copies, waits for them, and re-layouts: none -> 5.23 us  [jnp.stack([piece_in] * axis_size('dev'), axis=0)]
  transfers between devices with their start and end apart: 4 -> 4, of which waited for: 3 -> 3; matrix products, arithmetic and copies ran while one was open for 48% -> 43% of each run, Pallas kernels for 0% -> 0%
where the time goes in v1:
time: 358 us; the launch traced here: 357 us
  local copies, waits for them, and re-layouts  146 us (41%)
  waiting for transfers between devices  145 us (41%)
  starting transfers between devices  39.6 us (11%)
  between operations  13.6 us (4%)
  other arithmetic  10.8 us (3%)
    all_gather x1, waiting for transfers between devices, shards(): lax.all_gather(sub_factor, 'dev', axis=1, tiled=True)  112 us
    gather x1, local copies, waits for them, and re-layouts, one_block(): user_rows = jnp.take(user_table, users_block, axis=0).astype(jnp.float32)  62.9 us
    gather x1, local copies, waits for them, and re-layouts, one_block(): sub_rows = jnp.take(sub_table, subs_block, axis=0).astype(jnp.float32)  57.7 us
    all_to_all x2, starting transfers between devices, exchange_both(): lax.all_to_all(pieces, axis, split_axis=0, concat_axis=0, tiled=True)  26.3 us
    all_to_all x1, waiting for transfers between devices, all_to_all(jnp.stack([piece_in] * axis_size('dev'), axis=0), 'dev', 0, 0)  21.1 us
    reshape x1, local copies, waits for them, and re-layouts, jnp.concatenate(all_to_all(jnp.stack([piece_in] * axis_size('dev'), axis=...  15.5 us
    all_to_all x1, starting transfers between devices, all_to_all(jnp.stack([piece_in] * axis_size('dev'), axis=0), 'dev', 0, 0)  13.3 us
    all_to_all x2, waiting for transfers between devices, exchange_both(): lax.all_to_all(pieces, axis, split_axis=0, concat_axis=0, tiled=True)  11.5 us
  transfers between devices with their start and end apart: 4, of which 3 were waited for; matrix products, arithmetic and copies ran while one was open for 43% of the time, Pallas kernels for 0%

profile of v1, /device:TPU:1, one launch (start us, length us, event | category | flops | bytes accessed | tf_op | source)
XLA Modules:
  0.0 357.3 jit_solution(3798404651440714828)
XLA Ops:
  6.5 5.2 %stack.2 = bf16[64,64,1024]{2,1,0:T(8,128)(2,1)} broadcast(bf16[64,1024]{1,0:T(8,128)(2,1)} %param.12), dimensions={1,2} | broadcast | bytes 8519680 | tf_op jit(solution)/shard_map/stack | solution.py:9
  11.8 13.3 %all-to-all-start = ((bf16[64,64,1024]{2,1,0:T(8,128)(2,1)}), bf16[64,64,1024]{2,1,0:T(8,128)(2,1)}, u32[]{:S(2)}, u32[]{:S(2)}) async-start(bf16[64,64,1024]{2,1,0:T(8,128)(2,1)} %stack.2), calls=%async_computation | async-start | bytes 16777216 | tf_op jit(solution)/shard_map/all_to_all | solution.py:9
  25.2 0.7 copy.45
  26.0 1.1 gather_fusion.2
  27.1 0.3 fusion
  27.6 0.3 fusion.1
  27.9 0.1 reshape_reshape.14
  28.0 0.7 copy.55
  28.9 112.2 %all-gather.2.cloned.1.call-done = bf16[64,16384]{0,1:T(8,128)(2,1)} async-done(((bf16[64,256]{0,1:T(8,128)(2,1)}), bf16[64,16384]{0,1:T(8,128)(2,1)}) %all-gather.2.cloned.1.call-update) | async-done | bytes 2097168 | tf_op jit(solution)/shard_map/all_gather | solution.py:61
  141.1 57.7 %gather_fusion.1 = bf16[16384,64]{1,0:T(8,128)(2,1)} fusion(bf16[16384,64]{1,0:T(8,128)(2,1)} %bitcast.41, s32[16384]{0:T(1024)S(1)} %bitcast_clamp_fusion), kind=kCustom, calls=%fused_computation.1 | custom fusion | bytes 4259840 | tf_op jit(solution)/shard_map/while/body/eval_jaxpr/jit(_take)/gather | solution.py:44
  198.7 21.1 %all-to-all-done = bf16[64,64,1024]{2,1,0:T(8,128)(2,1)} async-done(((bf16[64,64,1024]{2,1,0:T(8,128)(2,1)}), bf16[64,64,1024]{2,1,0:T(8,128)(2,1)}, u32[]{:S(2)}, u32[]{:S(2)}) %all-to-all-start) | async-done | bytes 8388640 | tf_op jit(solution)/shard_map/all_to_all | solution.py:9
  219.9 12.6 %all-to-all-start.2 = ((f32[256,1,1,2]{3,2,1,0:T(1,128)}), f32[256,1,1,2]{3,2,1,0:T(1,128)S(1)}, u32[]{:S(2)}, u32[]{:S(2)}) async-start(f32[256,1,1,2]{3,2,1,0:T(1,128)} %bitcast.16), calls=%async_computation.2 | async-start | bytes 262144 | tf_op jit(solution)/shard_map/all_to_all | solution.py:31
  232.4 15.5 %copy.44 = bf16[64,64,1024]{0,2,1:T(8,128)(2,1)} copy(bf16[64,64,1024]{2,0,1:T(8,128)(2,1)} %bitcast) | data formatting | bytes 16777216 | tf_op jit(solution)/shard_map/reshape | solution.py:8
  248.0 62.9 %gather_fusion = bf16[16384,64]{1,0:T(8,128)(2,1)} fusion(bf16[65536,64]{1,0:T(8,128)(2,1)} %bitcast.42, s32[16384]{0:T(1024)S(1)} %bitcast_clamp_fusion.1), kind=kCustom, calls=%fused_computation | custom fusion | bytes 4259840 | tf_op jit(solution)/shard_map/while/body/eval_jaxpr/jit(_take)/gather | solution.py:43
  310.9 10.6 %multiply_reduce_fusion = f32[128,64]{1,0:T(8,128)S(1)} fusion(f32[128,128]{1,0:T(8,128)S(1)} %copy-done.3, pred[128,128]{1,0:T(8,128)(4,1)S(1)} %get-tuple-element.30, pred[128,128]{1,0:T(8,128)(4,1)S(1)} %get-tuple-element.32, bf16[16384,64]{1,0:T(8,128)(2,1)} %gather_fusion.1, bf16[16384,64]{1,0:T(8,128)(2,1)} %gather_fusion), kind=kLoop, calls=%fused_computation.3 | loop fusion | flops 7331840 | bytes 4325376 | tf_op jit(solution)/shard_map/while/body/eval_jaxpr/reduce_sum | solution.py:45
  321.5 0.5 fusion.2
  322.0 0.7 copy.47
  322.8 13.7 %all-to-all-start.1 = ((f32[256,1,1,128]{3,2,1,0:T(1,128)}), f32[256,1,1,128]{3,2,1,0:T(1,128)S(1)}, u32[]{:S(2)}, u32[]{:S(2)}) async-start(f32[256,1,1,128]{3,2,1,0:T(1,128)} %bitcast.10), calls=%async_computation.1 | async-start | bytes 262144 | tf_op jit(solution)/shard_map/all_to_all | solution.py:31
  336.6 0.1 convert_element_type.45
  336.7 0.6 copy.53
  337.3 0.2 convert_element_type.47
  337.4 0.3 fusion.11
  337.7 11.5 %all-to-all-done.1 = f32[256,1,1,128]{3,2,1,0:T(1,128)S(1)} async-done(((f32[256,1,1,128]{3,2,1,0:T(1,128)}), f32[256,1,1,128]{3,2,1,0:T(1,128)S(1)}, u32[]{:S(2)}, u32[]{:S(2)}) %all-to-all-start.1) | async-done | bytes 131104 | tf_op jit(solution)/shard_map/all_to_all | solution.py:31
  349.3 1.1 convolution_add_fusion
  (29 shorter events, 0.6 us)
Async XLA Ops:
  6.5 19.4 %copy-start = (s32[16384]{0:T(1024)S(1)}, s32[16384]{0:T(1024)}, u32[]{:S(2)}) copy-start(s32[16384]{0:T(1024)} %param.11) | copy-start | bytes 196612
  11.8 13.4 %copy-start.4 = (bf16[64,256]{1,0:T(8,128)(2,1)S(1)}, bf16[64,256]{1,0:T(8,128)(2,1)}, u32[]{:S(2)}) copy-start(bf16[64,256]{1,0:T(8,128)(2,1)} %param.13) | copy-start | bytes 98308
  11.8 14.1 %copy-start.5 = (s32[128]{0:T(128)S(1)}, s32[128]{0:T(128)}, u32[]{:S(2)}) copy-start(s32[128]{0:T(128)} %param.10) | copy-start | bytes 1540
  11.8 17.0 %copy-start.1 = (s32[128,128]{1,0:T(8,128)S(1)}, s32[128,128]{1,0:T(8,128)}, u32[]{:S(2)}) copy-start(s32[128,128]{1,0:T(8,128)} %param.7) | copy-start | bytes 196612
  11.8 17.0 %copy-start.2 = (s32[128,128]{1,0:T(8,128)S(1)}, s32[128,128]{1,0:T(8,128)}, u32[]{:S(2)}) copy-start(s32[128,128]{1,0:T(8,128)} %param.8) | copy-start | bytes 196612
  11.8 208.1 %all-to-all-start = ((bf16[64,64,1024]{2,1,0:T(8,128)(2,1)}), bf16[64,64,1024]{2,1,0:T(8,128)(2,1)}, u32[]{:S(2)}, u32[]{:S(2)}) async-start(bf16[64,64,1024]{2,1,0:T(8,128)(2,1)} %stack.2), calls=%async_computation | async-start | bytes 16777216 | tf_op jit(solution)/shard_map/all_to_all | solution.py:9
  25.1 116.0 %all-gather.2.cloned.1.call-start = ((), (), s32[]{:S(2)}) async-start(), calls=%async_computation.3 | async-start | bytes 4259840 | tf_op jit(solution)/shard_map/all_gather | solution.py:61
  219.9 102.9 %all-to-all-start.2 = ((f32[256,1,1,2]{3,2,1,0:T(1,128)}), f32[256,1,1,2]{3,2,1,0:T(1,128)S(1)}, u32[]{:S(2)}, u32[]{:S(2)}) async-start(f32[256,1,1,2]{3,2,1,0:T(1,128)} %bitcast.16), calls=%async_computation.2 | async-start | bytes 262144 | tf_op jit(solution)/shard_map/all_to_all | solution.py:31
  248.0 62.9 %copy-start.3 = (f32[128,128]{1,0:T(8,128)S(1)}, f32[128,128]{1,0:T(8,128)}, u32[]{:S(2)}) copy-start(f32[128,128]{1,0:T(8,128)} %param.9) | copy-start | bytes 196612
  322.8 26.4 %all-to-all-start.1 = ((f32[256,1,1,128]{3,2,1,0:T(1,128)}), f32[256,1,1,128]{3,2,1,0:T(1,128)S(1)}, u32[]{:S(2)}, u32[]{:S(2)}) async-start(f32[256,1,1,128]{3,2,1,0:T(1,128)} %bitcast.10), calls=%async_computation.1 | async-start | bytes 262144 | tf_op jit(solution)/shard_map/all_to_all | solution.py:31
Sparse Core Ops, SparseCore 0:
  28.7 112.3 all-gather.1
